TPU v7x, 32 devices: a whole 2x2x4 slice. The times are simulated.
32 devices in a mesh: py: 8 (over y, x, core), px: 4 (over z).
Axes of the slice: x: 2, y: 2, z: 4, core: 2. Of those that a mesh axis runs over, the one named last changes fastest.
Arguments:
- source_terms: float32 [512, 512, 256], P('py', 'px'), may hold values from -6 to 6
- initial_values: float32 [512, 512, 256], P('py', 'px'), may hold values from -6 to 6
- absorption: float32 [512, 512, 256], P('py', 'px'), may hold values from 0.1 to 0.9
Outputs:
- improved: float32 [512, 512, 256], P('py', 'px')
All inputs are finite; a program needn't handle non-finite values.
Results may differ from a plain program's by a relative error of at most 0.00002.
Values sent between devices are 32-bit elements; how exact they have to be, the bound alone decides.
A program may use at most 128 MiB of HBM per device.

v0:
```python
import functools

import jax
import jax.numpy as jnp
from jax import lax
from jax.experimental import pallas as pl
from jax.experimental.pallas import tpu as pltpu
from jax.sharding import PartitionSpec as P

RATIO = 4
INNER = 13
LANES = 128
DEEP = 7
MESH = pl.DeviceIdType.MESH
CHUNKS = 4


def kernel(shape, s_hbm, u_hbm, a_hbm, out_hbm, U, V, S, Q, R, D, CL, CR, CA, CB, CE, SP,
           RR, RC, PC, in_sem, out_sem, fs_sem, fr_sem, cs_sem, cr_sem):
    H, W, halves = shape
    HC, WC = H // RATIO, W // RATIO
    XW = W + 16
    npy, npx = lax.axis_size("py"), lax.axis_size("px")
    py, px = lax.axis_index("py"), lax.axis_index("px")
    ypos = {-1: lax.rem(py + npy - 1, npy), 0: py, 1: lax.rem(py + 1, npy)}
    xpos = {-1: lax.rem(px + npx - 1, npx), 0: px, 1: lax.rem(px + 1, npx)}
    eight = [(dy, dx) for dy in (-1, 0, 1) for dx in (-1, 0, 1) if dy or dx]

    def load(hbm, dst, row0, rows, half, sem):
        return pltpu.make_async_copy(
            hbm.at[pl.ds(row0, rows), :, pl.ds(half * LANES, LANES)], dst, sem)

    u_loads = [load(u_hbm, U.at[h, pl.ds(1, H), pl.ds(8, W), :], 0, H, h, in_sem.at[0, 0, h])
               for h in range(halves)]
    for c in u_loads:
        c.start()
    step = H // CHUNKS
    chunk_loads = []
    for k in range(CHUNKS):
        row = []
        for h in range(halves):
            row.append(load(a_hbm, Q.at[h, pl.ds(k * step, step)], k * step, step, h,
                            in_sem.at[1, k, h]))
        for c in row:
            c.start()
        chunk_loads.append(row)
    s_loads = [load(s_hbm, S.at[h], 0, H, h, in_sem.at[2, 0, h]) for h in range(halves)]
    for c in s_loads:
        c.start()

    barrier = pltpu.get_barrier_semaphore()
    for dy, dx in eight:
        pl.semaphore_signal(barrier, inc=1, device_id={"py": ypos[dy], "px": xpos[dx]},
                            device_id_type=MESH)
    pl.semaphore_wait(barrier, 8)

    def flat(buf):
        return buf.reshape(halves * (H + 2) * XW, LANES)

    def send_fine(buf, k):
        rows = []
        for n, (dy, row) in enumerate(((-1, 1), (1, H))):
            c = pltpu.make_async_remote_copy(
                src_ref=buf.at[:, row, pl.ds(8, W), :], dst_ref=RR.at[k, n],
                send_sem=fs_sem.at[k, n], recv_sem=fr_sem.at[k, n],
                device_id={"py": ypos[dy], "px": px}, device_id_type=MESH)
            c.start()
            rows.append(c)
        f = flat(buf)
        for n, (dx, col) in enumerate(((-1, 8), (1, 7 + W))):
            for h in range(halves):
                for g in range(0, H, 8):
                    PC[k, n, h, g:g + 8, :] = f[
                        pl.ds((h * (H + 2) + 1 + g) * XW + col, 8, stride=XW), :]
            c = pltpu.make_async_remote_copy(
                src_ref=PC.at[k, n], dst_ref=RC.at[k, n],
                send_sem=fs_sem.at[k, 2 + n], recv_sem=fr_sem.at[k, 2 + n],
                device_id={"py": py, "px": xpos[dx]}, device_id_type=MESH)
            c.start()
            rows.append(c)
        return rows

    def land_fine(buf, k, copies):
        for c in copies:
            c.wait()
        for n, row in enumerate((H + 1, 0)):
            for h in range(halves):
                buf[h, row, 8:8 + W, :] = RR[k, n, h]
        f = flat(buf)
        for n, col in enumerate((8 + W, 7)):
            for h in range(halves):
                for g in range(0, H, 8):
                    f[pl.ds((h * (H + 2) + 1 + g) * XW + col, 8, stride=XW), :] = (
                        RC[k, n, h, g:g + 8, :])

    def around(buf, h, Y, x):
        base = RATIO * Y
        c = [buf[h, base + i, x:x + 8, :] for i in range(RATIO + 2)]
        for i in range(RATIO):
            left = buf[h, base + 1 + i, x - 1:x + 7, :]
            right = buf[h, base + 1 + i, x + 1:x + 9, :]
            yield base + i, c[i + 1], (c[i] + c[i + 2]) + (left + right)

    def relax(src, dst):
        def unit(h, Y, x):
            for y, mid, nb in around(src, h, Y, x):
                dst[h, y + 1, x:x + 8, :] = (
                    0.2 * mid + (S[h, y, x - 8:x, :] + nb) * R[h, y, x - 8:x, :])
        return unit

    def defect(src):
        def unit(h, Y, x):
            total = None
            for y, mid, nb in around(src, h, Y, x):
                d = (S[h, y, x - 8:x, :] + nb) - Q[h, y, x - 8:x, :] * mid
                total = d if total is None else total + d
            D[h, Y, x - 8:x, :] = total
        return unit

    def inner(unit):
        @pl.loop(0, halves * (HC - 2))
        def _(i):
            h, Y = i // (HC - 2), 1 + i % (HC - 2)
            for x in range(16, W, 8):
                unit(h, Y, x)

    def rim(unit):
        @pl.loop(0, halves * 2)
        def _(i):
            h, Y = i // 2, (i % 2) * (HC - 1)
            for x in range(8, W + 8, 8):
                unit(h, Y, x)

        @pl.loop(0, halves * (HC - 2))
        def _(i):
            h, Y = i // (HC - 2), 1 + i % (HC - 2)
            unit(h, Y, 8)
            unit(h, Y, W)

    def reduce_into(dst, f):
        @pl.loop(0, halves * HC)
        def _(i):
            h, Y = i // HC, i % HC
            t = D[h, Y, pl.ds(0, WC, stride=RATIO), :]
            for k in range(1, RATIO):
                t = t + D[h, Y, pl.ds(k, WC, stride=RATIO), :]
            dst[h, DEEP + Y, 16:16 + WC, :] = f(t)

    ysrc = {-1: (DEEP, DEEP), 0: (DEEP, HC), 1: (HC, DEEP)}
    ydst = {-1: (DEEP + HC, DEEP), 0: (DEEP, HC), 1: (0, DEEP)}
    xsrc = {-1: (16, 8), 0: (16, WC), 1: (8 + WC, 8)}
    xdst = {-1: (16 + WC, 8), 0: (16, WC), 1: (8, 8)}

    def send_coarse(buf, k):
        copies = []
        for n, (dy, dx) in enumerate(eight):
            c = pltpu.make_async_remote_copy(
                src_ref=buf.at[:, pl.ds(*ysrc[dy]), pl.ds(*xsrc[dx]), :],
                dst_ref=buf.at[:, pl.ds(*ydst[dy]), pl.ds(*xdst[dx]), :],
                send_sem=cs_sem.at[k, n], recv_sem=cr_sem.at[k, n],
                device_id={"py": ypos[dy], "px": xpos[dx]}, device_id_type=MESH)
            c.start()
            copies.append(c)
        return copies

    def relax_coarse(src, dst, low, high, xlow, xhigh):
        @pl.loop(0, halves)
        def _(h):
            @pl.loop(low, high)
            def _(y):
                for x in range(xlow, xhigh, 8):
                    nb = (src[h, y - 1, x:x + 8, :] + src[h, y + 1, x:x + 8, :]) + (
                        src[h, y, x - 1:x + 7, :] + src[h, y, x + 1:x + 9, :])
                    dst[h, y, x:x + 8, :] = 0.2 * src[h, y, x:x + 8, :] + (
                        CL[h, y, x:x + 8, :] + nb) * CR[h, y, x:x + 8, :]

    for c in u_loads:
        c.wait()
    fine0 = send_fine(U, 0)
    for k in range(CHUNKS):
        for c in chunk_loads[k]:
            c.wait()
        groups = step // RATIO

        @pl.loop(0, halves * groups)
        def _(i):
            h, Y = i // groups, k * groups + i % groups
            for x in range(0, W, 8):
                total = None
                for j in range(RATIO):
                    m = Q[h, RATIO * Y + j, x:x + 8, :]
                    total = m if total is None else total + m
                    q = 4.0 + m
                    Q[h, RATIO * Y + j, x:x + 8, :] = q
                    R[h, RATIO * Y + j, x:x + 8, :] = 0.8 / q
                D[h, Y, x:x + 8, :] = total

    reduce_into(CR, lambda t: 0.8 / (4.0 + 0.25 * t))
    masses = send_coarse(CR, 0)
    for c in s_loads:
        c.wait()
    inner(relax(U, V))
    land_fine(U, 0, fine0)
    rim(relax(U, V))
    fine1 = send_fine(V, 1)
    inner(relax(V, U))
    land_fine(V, 1, fine1)
    rim(relax(V, U))
    fine2 = send_fine(U, 2)
    inner(defect(U))
    land_fine(U, 2, fine2)
    rim(defect(U))

    reduce_into(CL, lambda t: 0.25 * t)
    for c in masses:
        c.wait()
    loads = send_coarse(CL, 1)
    for c in loads:
        c.wait()
    TOP = HC + 2 * DEEP

    @pl.loop(0, halves)
    def _(h):
        @pl.loop(0, TOP)
        def _(y):
            CA[h, y, 8:24 + WC, :] = CL[h, y, 8:24 + WC, :] * CR[h, y, 8:24 + WC, :]

    src, dst = CA, CB
    for n in range(1, DEEP):
        last = n == DEEP - 1
        if last:
            relax_coarse(src, CE, DEEP, DEEP + HC, 16, 16 + WC)
        else:
            relax_coarse(src, dst, n, TOP - n, 8, 24 + WC)
            src, dst = dst, src
    values = send_coarse(CE, 2)
    for c in values:
        c.wait()
    src, dst = CE, CA
    spare = [CA, CB]
    for n in range(1, INNER - DEEP + 1):
        dst = spare[n % 2]
        relax_coarse(src, dst, n, TOP - n, 8, 24 + WC)
        src = dst
    coarse = src

    def add_coarse(h, Yc, rows):
        for k in range(RATIO):
            SP[pl.ds(k, WC + 8, stride=RATIO), :] = coarse[h, Yc, 14:14 + WC + 8, :]
        for row in rows:
            for x in range(0, XW, 8):
                V[h, row, x:x + 8, :] = U[h, row, x:x + 8, :] + SP[x:x + 8, :]

    @pl.loop(0, halves)
    def _(h):
        add_coarse(h, DEEP - 1, [0])
        add_coarse(h, DEEP + HC, [H + 1])

    @pl.loop(0, halves * HC)
    def _(i):
        h, Y = i // HC, i % HC
        add_coarse(h, DEEP + Y, [RATIO * Y + 1 + j for j in range(RATIO)])

    rim(relax(V, U))
    fine3 = send_fine(U, 3)
    inner(relax(V, U))
    inner(relax(U, V))
    land_fine(U, 3, fine3)
    rim(relax(U, V))
    outs = [pltpu.make_async_copy(
        V.at[h, pl.ds(1, H), pl.ds(8, W), :], out_hbm.at[:, :, pl.ds(h * LANES, LANES)],
        out_sem.at[h]) for h in range(halves)]
    for c in outs:
        c.start()
    for c in outs:
        c.wait()


def local(source_terms, initial_values, absorption):
    H, W, cases = source_terms.shape
    halves = cases // LANES
    HC, WC = H // RATIO, W // RATIO
    f32 = jnp.float32
    coarse = pltpu.VMEM((halves, HC + 2 * DEEP, WC + 32, LANES), f32)
    fine = pltpu.VMEM((halves, H + 2, W + 16, LANES), f32)
    plain = pltpu.VMEM((halves, H, W, LANES), f32)
    hbm = pl.BlockSpec(memory_space=pl.ANY)
    return pl.pallas_call(
        functools.partial(kernel, (H, W, halves)),
        out_shape=jax.ShapeDtypeStruct((H, W, cases), f32),
        in_specs=[hbm] * 3,
        out_specs=hbm,
        scratch_shapes=[
            fine, fine, plain, plain, plain,
            pltpu.VMEM((halves, HC, W, LANES), f32),
            coarse, coarse, coarse, coarse, coarse,
            pltpu.VMEM((W + 32, LANES), f32),
            pltpu.VMEM((4, 2, halves, W, LANES), f32),
            pltpu.VMEM((4, 2, halves, H, LANES), f32),
            pltpu.VMEM((4, 2, halves, H, LANES), f32),
            pltpu.SemaphoreType.DMA((3, CHUNKS, halves)),
            pltpu.SemaphoreType.DMA((halves,)),
            pltpu.SemaphoreType.DMA((4, 4)),
            pltpu.SemaphoreType.DMA((4, 4)),
            pltpu.SemaphoreType.DMA((3, 8)),
            pltpu.SemaphoreType.DMA((3, 8)),
        ],
        compiler_params=pltpu.CompilerParams(
            collective_id=0, has_side_effects=True, vmem_limit_bytes=63 * 1024 * 1024),
        name="two_grid",
    )(source_terms, initial_values, absorption)


def solution(mesh):
    return jax.shard_map(
        local,
        mesh=mesh,
        in_specs=(P("py", "px", None), P("py", "px", None), P("py", "px", None)),
        out_specs=P("py", "px", None),
        check_vma=False,
    )
```

profile of v0, /device:TPU:0, one launch (start us, length us, event | category | flops | bytes accessed | tf_op | source)
XLA Modules:
  0.0 88.5 jit_solution(13888492055865691648)
XLA Ops:
  0.0 80.7 %two_grid.1 = f32[64,128,256]{2,1,0:T(8,128)} custom-call(f32[64,128,256]{2,1,0:T(8,128)} %s_hbm.1, f32[64,128,256]{2,1,0:T(8,128)} %u_hbm.1, f32[64,128,256]{2,1,0:T(8,128)} %a_hbm.1), custom_call_target="tpu_custom_call" | custom-call | tf_op jit(solution)/shard_map/two_grid/pallas_call | solution.py:288
  80.7 7.8 %copy.5 = f32[64,128,256]{2,1,0:T(8,128)} copy(f32[64,128,256]{2,1,0:T(8,128)} %two_grid.1) | data formatting | bytes 16777216
where the time goes:
time: 88.6 us; the launch traced here: 88.5 us
  Pallas kernels  80.7 us (91%)
  local copies, waits for them, and re-layouts  7.77 us (9%)
    pallas_call x1, Pallas kernels, local(): pl.pallas_call(functools.partial(kernel, (H, W, halves)), out_shape=jax.S...  80.7 us
    unnamed x1, local copies, waits for them, and re-layouts  7.77 us

commit v1 on v0

--- a/solution.py
+++ b/solution.py
@@ -15,8 +15,8 @@
 CHUNKS = 4
 
 
-def kernel(shape, s_hbm, u_hbm, a_hbm, out_hbm, U, V, S, Q, R, D, CL, CR, CA, CB, CE, SP,
-           RR, RC, PC, in_sem, out_sem, fs_sem, fr_sem, cs_sem, cr_sem):
+def kernel(shape, s_hbm, u_hbm, a_hbm, out, U, V, S, R, D, CL, CR, CA, CB, CE, SP,
+           RR, RC, PC, in_sem, fs_sem, fr_sem, cs_sem, cr_sem):
     H, W, halves = shape
     HC, WC = H // RATIO, W // RATIO
     XW = W + 16
@@ -38,9 +38,8 @@
     chunk_loads = []
     for k in range(CHUNKS):
         row = []
-        for h in range(halves):
-            row.append(load(a_hbm, Q.at[h, pl.ds(k * step, step)], k * step, step, h,
-                            in_sem.at[1, k, h]))
+        rows = pl.ds(k * step, step)
+        row.append(pltpu.make_async_copy(a_hbm.at[rows], out.at[rows], in_sem.at[1, k, 0]))
         for c in row:
             c.start()
         chunk_loads.append(row)
@@ -93,6 +92,9 @@
                     f[pl.ds((h * (H + 2) + 1 + g) * XW + col, 8, stride=XW), :] = (
                         RC[k, n, h, g:g + 8, :])
 
+    def lanes(h):
+        return pl.ds(pl.multiple_of(h * LANES, LANES), LANES)
+
     def around(buf, h, Y, x):
         base = RATIO * Y
         c = [buf[h, base + i, x:x + 8, :] for i in range(RATIO + 2)]
@@ -101,18 +103,21 @@
             right = buf[h, base + 1 + i, x + 1:x + 9, :]
             yield base + i, c[i + 1], (c[i] + c[i + 2]) + (left + right)
 
-    def relax(src, dst):
+    def relax(src, dst=None):
         def unit(h, Y, x):
             for y, mid, nb in around(src, h, Y, x):
-                dst[h, y + 1, x:x + 8, :] = (
-                    0.2 * mid + (S[h, y, x - 8:x, :] + nb) * R[h, y, x - 8:x, :])
+                new = 0.2 * mid + (S[h, y, x - 8:x, :] + nb) * R[h, y, x - 8:x, :]
+                if dst is None:
+                    out[y, x - 8:x, lanes(h)] = new
+                else:
+                    dst[h, y + 1, x:x + 8, :] = new
         return unit
 
     def defect(src):
         def unit(h, Y, x):
             total = None
             for y, mid, nb in around(src, h, Y, x):
-                d = (S[h, y, x - 8:x, :] + nb) - Q[h, y, x - 8:x, :] * mid
+                d = (S[h, y, x - 8:x, :] + nb) - out[y, x - 8:x, lanes(h)] * mid
                 total = d if total is None else total + d
             D[h, Y, x - 8:x, :] = total
         return unit
@@ -164,15 +169,17 @@
         return copies
 
     def relax_coarse(src, dst, low, high, xlow, xhigh):
-        @pl.loop(0, halves)
-        def _(h):
-            @pl.loop(low, high)
-            def _(y):
+        @pl.loop(0, (high - low) // 2)
+        def _(i):
+            y = low + 2 * i
+            for h in range(halves):
                 for x in range(xlow, xhigh, 8):
-                    nb = (src[h, y - 1, x:x + 8, :] + src[h, y + 1, x:x + 8, :]) + (
-                        src[h, y, x - 1:x + 7, :] + src[h, y, x + 1:x + 9, :])
-                    dst[h, y, x:x + 8, :] = 0.2 * src[h, y, x:x + 8, :] + (
-                        CL[h, y, x:x + 8, :] + nb) * CR[h, y, x:x + 8, :]
+                    c = [src[h, y - 1 + j, x:x + 8, :] for j in range(4)]
+                    for j in range(2):
+                        nb = (c[j] + c[j + 2]) + (
+                            src[h, y + j, x - 1:x + 7, :] + src[h, y + j, x + 1:x + 9, :])
+                        dst[h, y + j, x:x + 8, :] = 0.2 * c[j + 1] + (
+                            CL[h, y + j, x:x + 8, :] + nb) * CR[h, y + j, x:x + 8, :]
 
     for c in u_loads:
         c.wait()
@@ -188,10 +195,10 @@
             for x in range(0, W, 8):
                 total = None
                 for j in range(RATIO):
-                    m = Q[h, RATIO * Y + j, x:x + 8, :]
+                    m = out[RATIO * Y + j, x:x + 8, lanes(h)]
                     total = m if total is None else total + m
                     q = 4.0 + m
-                    Q[h, RATIO * Y + j, x:x + 8, :] = q
+                    out[RATIO * Y + j, x:x + 8, lanes(h)] = q
                     R[h, RATIO * Y + j, x:x + 8, :] = 0.8 / q
                 D[h, Y, x:x + 8, :] = total
 
@@ -264,16 +271,9 @@
     rim(relax(V, U))
     fine3 = send_fine(U, 3)
     inner(relax(V, U))
-    inner(relax(U, V))
+    inner(relax(U))
     land_fine(U, 3, fine3)
-    rim(relax(U, V))
-    outs = [pltpu.make_async_copy(
-        V.at[h, pl.ds(1, H), pl.ds(8, W), :], out_hbm.at[:, :, pl.ds(h * LANES, LANES)],
-        out_sem.at[h]) for h in range(halves)]
-    for c in outs:
-        c.start()
-    for c in outs:
-        c.wait()
+    rim(relax(U))
 
 
 def local(source_terms, initial_values, absorption):
@@ -287,11 +287,11 @@
     hbm = pl.BlockSpec(memory_space=pl.ANY)
     return pl.pallas_call(
         functools.partial(kernel, (H, W, halves)),
-        out_shape=jax.ShapeDtypeStruct((H, W, cases), f32),
+        out_shape=pltpu.VMEM((H, W, cases), f32),
         in_specs=[hbm] * 3,
-        out_specs=hbm,
+        out_specs=pl.BlockSpec(memory_space=pltpu.VMEM),
         scratch_shapes=[
-            fine, fine, plain, plain, plain,
+            fine, fine, plain, plain,
             pltpu.VMEM((halves, HC, W, LANES), f32),
             coarse, coarse, coarse, coarse, coarse,
             pltpu.VMEM((W + 32, LANES), f32),
@@ -299,14 +299,13 @@
             pltpu.VMEM((4, 2, halves, H, LANES), f32),
             pltpu.VMEM((4, 2, halves, H, LANES), f32),
             pltpu.SemaphoreType.DMA((3, CHUNKS, halves)),
-            pltpu.SemaphoreType.DMA((halves,)),
             pltpu.SemaphoreType.DMA((4, 4)),
             pltpu.SemaphoreType.DMA((4, 4)),
             pltpu.SemaphoreType.DMA((3, 8)),
             pltpu.SemaphoreType.DMA((3, 8)),
         ],
         compiler_params=pltpu.CompilerParams(
-            collective_id=0, has_side_effects=True, vmem_limit_bytes=63 * 1024 * 1024),
+            collective_id=0, has_side_effects=True, vmem_limit_bytes=52 * 1024 * 1024),
         name="two_grid",
     )(source_terms, initial_values, absorption)
 

time: 88.6 us -> 77.1 us (0.87)
  Pallas kernels: 80.7 us -> 73.6 us
  local copies, waits for them, and re-layouts: 7.77 us -> 3.4 us
    pallas_call x1, Pallas kernels: 80.7 us -> 73.6 us  [local(): pl.pallas_call(functools.partial(kernel, (H, W, halves)), out_shape=pltpu...]
    unnamed x1, local copies, waits for them, and re-layouts: 7.77 us -> 3.4 us
where the time goes in v1:
time: 77.1 us; the launch traced here: 77 us
  Pallas kernels  73.6 us (95%)
  local copies, waits for them, and re-layouts  3.4 us (4%)
    pallas_call x1, Pallas kernels, local(): pl.pallas_call(functools.partial(kernel, (H, W, halves)), out_shape=pltpu...  73.6 us
    unnamed x1, local copies, waits for them, and re-layouts  3.4 us

profile of v1, /device:TPU:0, one launch (start us, length us, event | category | flops | bytes accessed | tf_op | source)
XLA Modules:
  0.0 77.0 jit_solution(1419460155825632451)
XLA Ops:
  0.0 73.6 %two_grid.1 = f32[64,128,256]{2,1,0:T(8,128)S(1)} custom-call(f32[64,128,256]{2,1,0:T(8,128)} %s_hbm.1, f32[64,128,256]{2,1,0:T(8,128)} %u_hbm.1, f32[64,128,256]{2,1,0:T(8,128)} %a_hbm.1), custom_call_target="tpu_custom_call" | custom-call | tf_op jit(solution)/shard_map/two_grid/pallas_call | solution.py:288
  73.6 3.4 %copy.5 = f32[64,128,256]{2,1,0:T(8,128)} copy(f32[64,128,256]{2,1,0:T(8,128)S(1)} %two_grid.1) | data formatting | bytes 16777216
